TPU v7x, 512 devices: a whole 4x8x8 slice. The times are simulated.
512 devices in a mesh: replica: 32 (over z, x_hi, core), expert: 16 (over x_lo, y).
Axes of the slice: x: 4 (x_hi: 2, x_lo: 2; x = x_hi * 2 + x_lo), y: 8, z: 8, core: 2. Of those that a mesh axis runs over, the one named last changes fastest.
Arguments:
- tokens: float32 [98304, 2048], P(('replica', 'expert')), may hold values from -6 to 6
- expert_ids: int32 [98304, 2], P(('replica', 'expert')), may hold values from 0 to 15, all different within a row; in each aligned block of 192 rows (0 to 191, 192 to 383, ...) at most 36 rows name the same one
- combine_weights: float32 [98304, 2], P(('replica', 'expert')), may hold values from 0.3 to 1
- gate_weight: bfloat16 [16, 2048, 768], P('expert', 'replica'), may hold values from -0.125 to 0.125
- up_weight: bfloat16 [16, 2048, 768], P('expert', 'replica'), may hold values from -0.125 to 0.125
- down_weight: bfloat16 [16, 2048, 768], P('expert', 'replica'), may hold values from -0.21875 to 0.21875
- norm_gain: float32 [2048], replicated, may hold values from 0.1 to 1.9
Outputs:
- normed: float32 [98304, 2048], P(('replica', 'expert'))
Inputs may be any that keep to these rules, and one draw needn't show every extreme that they name: `expert_ids`: each row names two different experts. In each aligned block of 192 rows (the rows of one device) no expert is named by more than 36 rows, a bound that some block reaches.
All inputs are finite; a program needn't handle non-finite values.
Results may differ from a plain program's by a relative error of at most 0.0027.
Values may be sent and summed in bfloat16 or wider, within the bound.
A program may use at most 64 MiB of HBM per device.

v0:
```python
import jax
import jax.numpy as jnp
from jax import lax
from jax.sharding import PartitionSpec as P


def sent_together(arrays, axis, dim, along):
    both = jnp.concatenate(arrays, axis=along)
    out, at, gathered = (lax.all_gather(both, axis, axis=dim, tiled=True), 0, [])
    for a in arrays:
        gathered.append(lax.slice_in_dim(out, at, at + a.shape[along], axis=along))
        at += a.shape[along]
    return tuple(gathered)


def slot_positions(expert_ids, experts, capacity):
    count = expert_ids.shape[0]
    onehot = (expert_ids[:, :, None] == jnp.arange(experts, dtype=jnp.int32)[None, None, :]).astype(
        jnp.int32
    )
    onehot = onehot.reshape(count * 2, experts)
    before = jnp.cumsum(onehot, axis=0) - onehot
    ranks = jnp.sum(before * onehot, axis=1).reshape(count, 2)
    return expert_ids * capacity + ranks


def place_rows(tokens, slot_index, total):
    iota_slots = jnp.arange(total, dtype=jnp.int32)[:, None]
    select = (slot_index[None, :, 0] == iota_slots) | (slot_index[None, :, 1] == iota_slots)
    return jnp.dot(
        select.astype(jnp.bfloat16), tokens.astype(jnp.bfloat16), preferred_element_type=jnp.float32
    ).astype(jnp.bfloat16)


def expert_ffn(rows, gate, upward, downward):
    gate_out = jnp.dot(rows, gate, preferred_element_type=jnp.float32)
    up_out = jnp.dot(rows, upward, preferred_element_type=jnp.float32)
    hidden = (jax.nn.silu(gate_out) * up_out).astype(jnp.bfloat16)
    result = lax.dot_general(
        hidden, downward, (((1,), (1,)), ((), ())), preferred_element_type=jnp.float32
    )
    return result.astype(jnp.bfloat16)


def combine_rows(tokens, back, slot_index, weights, gain):
    picked = back[slot_index].astype(jnp.float32)
    summed = jnp.sum(picked * weights[:, :, None], axis=1)
    mixed = tokens + summed
    scale = lax.rsqrt(jnp.mean(mixed * mixed, axis=-1) + 1e-06)
    return mixed * scale[:, None] * gain[None, :]


def on_device(tokens, expert_ids, combine_weights, gate_weight, up_weight, down_weight, norm_gain):
    experts = lax.axis_size("expert")
    count = tokens.shape[0]
    width = tokens.shape[1]
    capacity = 3 * count // experts
    slot_index = slot_positions(expert_ids, experts, capacity)
    placed = place_rows(tokens, slot_index, experts * capacity).reshape(experts, capacity, width)
    gate_all, up_all, down_all = sent_together(
        (gate_weight, up_weight, down_weight), "replica", 1, 0
    )
    received = lax.all_to_all(placed, "expert", split_axis=0, concat_axis=0, tiled=True)
    sources = received.shape[0]
    items = received.shape[1]
    rows = received.reshape(sources * items, width)
    outs = expert_ffn(rows, gate_all[0], up_all[0], down_all[0])
    expert_out = outs.reshape(sources, items, width)
    back = lax.all_to_all(expert_out, "expert", split_axis=0, concat_axis=0, tiled=True)
    back = back.reshape(experts * capacity, width)
    return combine_rows(tokens, back, slot_index, combine_weights, norm_gain)


def solution(mesh):
    placed = (
        P(("replica", "expert"), None),
        P(("replica", "expert"), None),
        P(("replica", "expert"), None),
        P("expert", "replica", None),
        P("expert", "replica", None),
        P("expert", "replica", None),
        P(),
    )
    return jax.shard_map(
        on_device,
        mesh=mesh,
        in_specs=placed,
        out_specs=P(("replica", "expert"), None),
        check_vma=False,
    )
```

profile of v0, /device:TPU:1, one launch (start us, length us, event | category | flops | bytes accessed | tf_op | source)
XLA Modules:
  0.0 245.9 jit_solution(4074705585380352197)
XLA Ops:
  6.5 1.7 pad_maximum_fusion
  8.3 0.8 copy.21
  9.4 0.9 reduce-window.6
  10.3 0.2 slice_reduce_fusion
  10.6 0.1 reshape.43
  10.9 0.7 compare_select_fusion
  11.6 3.6 %convolution_convert_fusion = bf16[576,2048]{1,0:T(8,128)(2,1)} fusion(f32[192,2048]{1,0:T(8,128)} %param.7, s32[192]{0:T(256)S(1)} %bitcast.41, s32[192]{0:T(256)S(1)} %bitcast.40), kind=kOutput, calls=%fused_computation.9 | convolution fusion | flops 454889472 | bytes 3933696 | tf_op jit(solution)/shard_map/dot_general | solution.py:30
  15.1 2.6 %reshape.44 = bf16[16,36,2048]{2,1,0:T(8,128)(2,1)S(1)} reshape(bf16[576,2048]{1,0:T(8,128)(2,1)} %convolution_convert_fusion) | data formatting | bytes 4718592 | tf_op jit(solution)/shard_map/reshape | solution.py:59
  17.7 66.8 %all_to_all.10 = bf16[16,36,2048]{2,1,0:T(8,128)(2,1)} all-to-all(bf16[16,36,2048]{2,1,0:T(8,128)(2,1)S(1)} %reshape.44), channel_id=1, replica_groups=mesh['replica'=32,'expert'=16] {'expert'}, dimensions={0} | all-to-all | bytes 4718592 | tf_op jit(solution)/shard_map/all_to_all | solution.py:63
  84.6 2.7 %reshape.45 = bf16[576,2048]{1,0:T(8,128)(2,1)S(1)} reshape(bf16[16,36,2048]{2,1,0:T(8,128)(2,1)} %all_to_all.10) | data formatting | bytes 4718592 | tf_op jit(solution)/shard_map/reshape | solution.py:66
  87.3 51.6 %all-gather.2.cloned.1.call-done = bf16[3,2048,768]{2,1,0:T(8,128)(2,1)} async-done(((bf16[3,64,768]{2,1,0:T(8,128)(2,1)}), bf16[3,2048,768]{2,1,0:T(8,128)(2,1)}) %all-gather.2.cloned.1.call-update) | async-done | bytes 9437200 | tf_op jit(solution)/shard_map/all_gather | solution.py:9
  138.9 5.2 %fusion.2 = f32[576,768]{1,0:T(8,128)} fusion(bf16[576,2048]{1,0:T(8,128)(2,1)S(1)} %reshape.45, bf16[3,2048,768]{2,1,0:T(8,128)(2,1)} %all-gather.2.cloned.1.call-done), kind=kOutput, calls=%fused_computation.6 | convolution fusion | flops 1811939328 | bytes 7274496 | tf_op jit(solution)/shard_map/dot_general | solution.py:36
  144.1 9.2 %fusion.3 = bf16[576,2048]{1,0:T(8,128)(2,1)} fusion(bf16[3,2048,768]{2,1,0:T(8,128)(2,1)} %all-gather.2.cloned.1.call-done, f32[576,768]{1,0:T(8,128)} %fusion.2, bf16[576,2048]{1,0:T(8,128)(2,1)S(1)} %reshape.45), kind=kOutput, calls=%fused_computation.8 | convolution fusion | flops 3627712512 | bytes 12779520 | tf_op jit(solution)/shard_map/dot_general | solution.py:39
  153.3 4.1 %reshape.46 = bf16[16,36,2048]{2,1,0:T(8,128)(2,1)} reshape(bf16[576,2048]{1,0:T(8,128)(2,1)} %fusion.3) | data formatting | bytes 4718592 | tf_op jit(solution)/shard_map/reshape | solution.py:68
  157.4 6.1 %all-to-all-start.1 = ((bf16[16,36,2048]{2,1,0:T(8,128)(2,1)}), bf16[16,36,2048]{2,1,0:T(8,128)(2,1)}, u32[]{:S(2)}, u32[]{:S(2)}) async-start(bf16[16,36,2048]{2,1,0:T(8,128)(2,1)} %reshape.46), calls=%async_computation.1 | async-start | bytes 5242880 | tf_op jit(solution)/shard_map/all_to_all | solution.py:69
  163.6 0.1 reshape.50
  163.9 58.9 %all-to-all-done.1 = bf16[16,36,2048]{2,1,0:T(8,128)(2,1)} async-done(((bf16[16,36,2048]{2,1,0:T(8,128)(2,1)}), bf16[16,36,2048]{2,1,0:T(8,128)(2,1)}, u32[]{:S(2)}, u32[]{:S(2)}) %all-to-all-start.1) | async-done | bytes 2359328 | tf_op jit(solution)/shard_map/all_to_all | solution.py:69
  222.8 2.7 %reshape.47 = bf16[576,2048]{1,0:T(8,128)(2,1)S(1)} reshape(bf16[16,36,2048]{2,1,0:T(8,128)(2,1)} %all-to-all-done.1) | data formatting | bytes 4718592 | tf_op jit(solution)/shard_map/reshape | solution.py:70
  225.5 3.1 %gather_fusion = bf16[384,2048]{1,0:T(8,128)(2,1)} fusion(bf16[576,2048]{1,0:T(8,128)(2,1)S(1)} %reshape.47, s32[1024]{0:T(1024)S(1)} %pad_clamp_fusion), kind=kCustom, calls=%fused_computation | custom fusion | bytes 3147264 | tf_op jit(solution)/shard_map/gather | solution.py:46
  228.6 3.4 %reshape.58 = f32[192,2,2048]{2,1,0:T(2,128)S(1)} reshape(bf16[384,2048]{1,0:T(8,128)(2,1)} %gather_fusion) | data formatting | bytes 4718592 | tf_op jit(solution)/shard_map/convert_element_type | solution.py:46
  232.0 5.0 %multiply_reduce_fusion = f32[192,2048]{1,0:T(8,128)S(1)} fusion(f32[192,2,2048]{2,1,0:T(2,128)S(1)} %reshape.58, f32[192,2]{1,0:T(8,128)S(1)} %copy.26), kind=kLoop, calls=%fused_computation.7 | loop fusion | flops 1179648 | bytes 4720128 | tf_op jit(solution)/shard_map/reduce_sum | solution.py:47
  237.0 0.3 multiply_reduce_fusion.1
  237.3 0.4 copy-done.1
  237.7 1.3 multiply_multiply_fusion
  (18 shorter events, 0.8 us)
Async XLA Ops:
  6.5 132.4 %all-gather.2.cloned.1.call-start = ((), (), s32[]{:S(2)}) async-start(), calls=%async_computation.2 | async-start | bytes 9732096 | tf_op jit(solution)/shard_map/all_gather | solution.py:9
  157.3 6.4 %copy-start.2 = (f32[192,2]{0,1:T(2,128)S(1)}, f32[192,2]{0,1:T(2,128)}, u32[]{:S(2)}) copy-start(f32[192,2]{0,1:T(2,128)} %param.9) | copy-start | bytes 4612
  157.4 65.4 %all-to-all-start.1 = ((bf16[16,36,2048]{2,1,0:T(8,128)(2,1)}), bf16[16,36,2048]{2,1,0:T(8,128)(2,1)}, u32[]{:S(2)}, u32[]{:S(2)}) async-start(bf16[16,36,2048]{2,1,0:T(8,128)(2,1)} %reshape.46), calls=%async_computation.1 | async-start | bytes 5242880 | tf_op jit(solution)/shard_map/all_to_all | solution.py:69
  232.0 5.0 %copy-start = (f32[192,2048]{1,0:T(8,128)S(1)}, f32[192,2048]{1,0:T(8,128)}, u32[]{:S(2)}) copy-start(f32[192,2048]{1,0:T(8,128)} %param.7) | copy-start | bytes 4718596
  237.0 0.7 copy-start.1
Sparse Core Ops, SparseCore 0:
  10.6 128.2 all-gather.1
where the time goes:
time: 248 us; the launch traced here: 246 us
  waiting for transfers between devices  111 us (45%)
  blocking collectives  66.8 us (27%)
  local copies, waits for them, and re-layouts  20.9 us (8%)
  matrix products  17.9 us (7%)
  between operations  13.5 us (5%)
  other arithmetic  10 us (4%)
  starting transfers between devices  6.12 us (2%)
    all_to_all x1, blocking collectives, on_device(): lax.all_to_all(placed, 'expert', split_axis=0, concat_axis=0, tiled=True)  66.8 us
    all_to_all x1, waiting for transfers between devices, on_device(): lax.all_to_all(expert_out, 'expert', split_axis=0, concat_axis=0, tiled=T...  58.9 us
    all_gather x1, waiting for transfers between devices, sent_together(): lax.all_gather(both, axis, axis=dim, tiled=True)  51.6 us
    dot_general x1, matrix products, expert_ffn(): lax.dot_general(hidden, downward, (((1,), (1,)), ((), ())), preferred_ele...  9.18 us
    all_to_all x1, starting transfers between devices, on_device(): lax.all_to_all(expert_out, 'expert', split_axis=0, concat_axis=0, tiled=T...  6.12 us
    dot_general x1, matrix products, expert_ffn(): gate_out = jnp.dot(rows, gate, preferred_element_type=jnp.float32)  5.19 us
    reduce_sum x1, other arithmetic, combine_rows(): summed = jnp.sum(picked * weights[:, :, None], axis=1)  4.99 us
  transfers between devices with their start and end apart: 2, of which 2 were waited for; matrix products, arithmetic and copies ran while one was open for 5% of the time, Pallas kernels for 0%

commit v1 on v0

v1 whole, which is shorter than its diff:
```python
import jax
import jax.numpy as jnp
from jax import lax
from jax.experimental import pallas as pl
from jax.experimental.pallas import tpu as pltpu
from jax.sharding import PartitionSpec as P

MESH = pl.DeviceIdType.MESH
BF = jnp.bfloat16
F32 = jnp.float32

TOK = 192
WIDTH = 2048
FF = 768
CAP = 36
MAIN = 32
TAIL = CAP - MAIN
GROUPS = 4
COLS = WIDTH // GROUPS
ROWS = GROUPS * CAP
SHARD = 64
PIECES = 3


def hop_y(k, dx):
    far = 2 if dx < 2 else 6
    one = k * (2 - k) * (3 - k) // 2
    two = k * (k - 1) * (3 - k) // 2
    three = k * (k - 1) * (k - 2) // 6
    return one + 7 * two + far * three


def where_am_i():
    r = lax.axis_index("replica")
    e = lax.axis_index("expert")
    z = r // 4
    xh = (r // 2) % 2
    core = r % 2
    xl = e // 8
    y = e % 8
    return xh * 2 + xl, y, z, core


def device(x, y, z, core):
    return ((z * 2 + x // 2) * 2 + core, (x % 2) * 8 + y)


def partner_of(ids, x, y):
    host_x = (ids >> 3) + 2 * ((ids >> 2) & 1)
    dx = (host_x - x) & 3
    d4 = ((ids & 3) - y) & 3
    k = d4 ^ (d4 >> 1)
    return ((k - dx - 1) & 3) * 4 + dx


def iota(shape, dim):
    return lax.broadcasted_iota(jnp.int32, shape, dim)


def kernel(
    tok_hbm, ids_ref, idst_ref, cw_ref, gate_hbm, up_hbm, down_hbm,
    mixed_ref,
    tok, w, send, recv, eout, back, whi, wlo, thi, tlo,
    tok_sem, pre_send, pre_recv, ring_send, ring_recv, sib_send, sib_recv,
    out_send, out_recv, ret_send, ret_recv,
):
    x, y, z, core = where_am_i()
    xh = x // 2
    mine = z * 4 + xh * 2 + core
    home = xh == y // 4
    shards = (gate_hbm, up_hbm, down_hbm)

    tok_copy = pltpu.make_async_copy(tok_hbm, tok, tok_sem)
    tok_copy.start()

    offsets = [(dx, dy) for dx in range(4) for dy in (0, 1, 7)]
    offsets += [(0, 2), (0, 6), (1, 2), (2, 2), (2, 6), (3, 6)]
    offsets += [(0, 4), (2, 4)]
    greet = [device((x + dx) % 4, (y + dy) % 8, z, core) for dx, dy in offsets if (dx, dy) != (0, 0)]
    greet += [device(x, y, z, 1 - core), device(x, y, (z + 1) % 8, core), device(x, y, (z + 7) % 8, core)]
    barrier = pltpu.get_barrier_semaphore()
    for d in greet:
        pl.semaphore_signal(barrier, inc=1, device_id=d, device_id_type=MESH)
    pl.semaphore_wait(barrier, len(greet))

    def piece(slot, p):
        return w.at[slot, pl.ds(p * SHARD, SHARD), :]

    def push_own(p, d):
        pltpu.make_async_remote_copy(
            src_ref=shards[p].at[0], dst_ref=piece(mine, p),
            send_sem=pre_send, recv_sem=pre_recv.at[xh, p],
            device_id=d, device_id_type=MESH,
        ).start()

    @pl.when(home)
    def _():
        for p in range(PIECES):
            pltpu.make_async_copy(shards[p].at[0], piece(mine, p), pre_recv.at[xh, p]).start()
            push_own(p, device(x, (y + 4) % 8, z, core))

    @pl.when(jnp.logical_not(home))
    def _():
        for p in range(PIECES):
            push_own(p, device((x + 2) % 4, (y + 4) % 8, z, core))
            push_own(p, device((x + 2) % 4, y, z, core))

    tok_copy.wait()
    q0 = partner_of(idst_ref[0:1, :], x, y)
    q1 = partner_of(idst_ref[1:2, :], x, y)
    hot0 = (q0 == iota((16, TOK), 0)).astype(F32)
    hot1 = (q1 == iota((16, TOK), 0)).astype(F32)
    upper = (iota((TOK, TOK), 0) < iota((TOK, TOK), 1)).astype(BF)
    count = jnp.dot((hot0 + hot1).astype(BF), upper, preferred_element_type=F32)
    rank0 = jnp.sum(hot0 * count, axis=0, keepdims=True).astype(jnp.int32)
    rank1 = jnp.sum(hot1 * count, axis=0, keepdims=True).astype(jnp.int32)
    main0 = jnp.where(rank0 < MAIN, q0 * MAIN + rank0, -1)
    main1 = jnp.where(rank1 < MAIN, q1 * MAIN + rank1, -1)
    tail0 = jnp.where(rank0 < MAIN, -1000, q0 * 16 + rank0 - MAIN)
    tail1 = jnp.where(rank1 < MAIN, -1000, q1 * 16 + rank1 - MAIN)
    select = jnp.where((main0 == iota((16 * MAIN, TOK), 0)) | (main1 == iota((16 * MAIN, TOK), 0)), 1.0, 0.0).astype(BF)
    tails = jnp.zeros((256, COLS), F32)
    for c in range(GROUPS):
        tok_c = tok[:, c * COLS:(c + 1) * COLS].astype(BF)
        placed = jnp.dot(select, tok_c, preferred_element_type=F32).astype(BF)
        send[:, c * MAIN:(c + 1) * MAIN, :] = placed.reshape(16, MAIN, COLS)
        at = iota((256, TOK), 0) - 4 * c
        pick = jnp.where((tail0 == at) | (tail1 == at), 1.0, 0.0).astype(BF)
        tails += jnp.dot(pick, tok_c, preferred_element_type=F32)
    send[:, GROUPS * MAIN:, :] = tails.astype(BF).reshape(16, 16, COLS)

    def message(q, buf_from, buf_to, sem_from, sem_to, d):
        return pltpu.make_async_remote_copy(
            src_ref=buf_from.at[q], dst_ref=buf_to.at[q], send_sem=sem_from, recv_sem=sem_to,
            device_id=d, device_id_type=MESH,
        )

    for g in range(4):
        for dx in range(4):
            q = g * 4 + dx
            dy = hop_y((g + 1 + dx) % 4, dx)
            if (dx, dy) != (0, 0):
                message(q, send, recv, out_send, out_recv, device((x + dx) % 4, (y + dy) % 8, z, core)).start()
    recv[12] = send[12]

    p0 = partner_of(ids_ref[:, 0:1], x, y)
    p1 = partner_of(ids_ref[:, 1:2], x, y)
    col0 = (p0 == iota((TOK, 16), 1)).astype(F32)
    col1 = (p1 == iota((TOK, 16), 1)).astype(F32)
    lower = (iota((TOK, TOK), 1) < iota((TOK, TOK), 0)).astype(BF)
    ccount = jnp.dot(lower, (col0 + col1).astype(BF), preferred_element_type=F32)
    crank0 = jnp.sum(col0 * ccount, axis=1, keepdims=True).astype(jnp.int32)
    crank1 = jnp.sum(col1 * ccount, axis=1, keepdims=True).astype(jnp.int32)
    cw0 = cw_ref[:, 0:1]
    cw1 = cw_ref[:, 1:2]
    cmain0 = jnp.where(crank0 < MAIN, p0 * MAIN + crank0, -1)
    cmain1 = jnp.where(crank1 < MAIN, p1 * MAIN + crank1, -1)
    ctail0 = jnp.where(crank0 < MAIN, -1000, p0 * 16 + crank0 - MAIN)
    ctail1 = jnp.where(crank1 < MAIN, -1000, p1 * 16 + crank1 - MAIN)
    slots = iota((TOK, 16 * MAIN), 1)
    full = jnp.where(cmain0 == slots, cw0, 0.0) + jnp.where(cmain1 == slots, cw1, 0.0)
    high = full.astype(BF)
    whi[...] = high
    wlo[...] = (full - high.astype(F32)).astype(BF)
    for c in range(GROUPS):
        slots = iota((TOK, 256), 1) - 4 * c
        full = jnp.where(ctail0 == slots, cw0, 0.0) + jnp.where(ctail1 == slots, cw1, 0.0)
        high = full.astype(BF)
        thi[c] = high
        tlo[c] = (full - high.astype(F32)).astype(BF)

    def ring(step, way, hx, p, slot):
        d = device(x, y, (z + (1 if way == 0 else 7)) % 8, core)
        return pltpu.make_async_remote_copy(
            src_ref=piece(slot, p), dst_ref=piece(slot, p),
            send_sem=ring_send, recv_sem=ring_recv.at[((step * 2 + way) * 2 + hx) * PIECES + p],
            device_id=d, device_id_type=MESH,
        )

    def sibling(p, slot, from_z):
        return pltpu.make_async_remote_copy(
            src_ref=piece(slot, p), dst_ref=piece(slot, p),
            send_sem=sib_send, recv_sem=sib_recv.at[from_z],
            device_id=device(x, y, z, 1 - core), device_id_type=MESH,
        )

    for p in range(PIECES):
        for turn in range(2):
            hx = xh if turn == 0 else 1 - xh
            slot = z * 4 + hx * 2 + core
            pltpu.make_async_copy(piece(slot, p), piece(slot, p), pre_recv.at[hx, p]).wait()
            for way in range(2):
                d = device(x, y, (z + (1 if way == 0 else 7)) % 8, core)
                pltpu.make_async_remote_copy(
                    src_ref=piece(slot, p), dst_ref=piece(slot, p),
                    send_sem=ring_send, recv_sem=ring_recv.at[(way * 2 + hx) * PIECES + p],
                    device_id=d, device_id_type=MESH,
                ).start()
            sibling(p, slot, z).start()

    for step in range(4):
        for p in range(PIECES):
            for hx in range(2):
                for way in range(2):
                    if step == 3 and way != hx:
                        continue
                    origin = (z + (7 - step if way == 0 else 1 + step)) % 8
                    slot = origin * 4 + hx * 2 + core
                    ring(step, way, hx, p, slot).wait_recv()
                    if step < 2 or (step == 2 and way == hx):
                        ring(step + 1, way, hx, p, slot).start()
                    sibling(p, slot, origin).start()

    pltpu.make_async_copy(recv.at[0:15], recv.at[0:15], out_recv).wait()
    for k in range(8):
        pltpu.make_async_copy(w.at[0:2], w.at[0:2], sib_recv.at[k]).wait()

    def spread(c):
        a = iota((16, 64), 0)
        b = iota((16, 64), 1)
        return jnp.where((a // 4 == b // 16) & (a % 4 == b % 4) & ((b // 4) % 4 == c), 1.0, 0.0).astype(BF)

    def gather(c):
        a = iota((64, 16), 1)
        b = iota((64, 16), 0)
        return jnp.where((a // 4 == b // 16) & (a % 4 == b % 4) & ((b // 4) % 4 == c), 1.0, 0.0).astype(BF)

    def chunk(g, carry):
        base = pl.multiple_of(g * 4, 4)
        last = recv[pl.ds(base, 4), GROUPS * MAIN:, :].reshape(64, COLS)
        gate = jnp.zeros((4 * CAP, FF), F32)
        upward = jnp.zeros((4 * CAP, FF), F32)
        for c in range(GROUPS):
            main = recv[pl.ds(base, 4), c * MAIN:(c + 1) * MAIN, :].reshape(4 * MAIN, COLS)
            rest = jnp.dot(spread(c), last, preferred_element_type=F32).astype(BF)
            rows = jnp.concatenate([main, rest], axis=0)
            gate += jnp.dot(rows, w[c * 8:(c + 1) * 8, 0:SHARD, :].reshape(COLS, FF), preferred_element_type=F32)
            upward += jnp.dot(rows, w[c * 8:(c + 1) * 8, SHARD:2 * SHARD, :].reshape(COLS, FF), preferred_element_type=F32)
        hidden = (gate / (1.0 + jnp.exp(-gate)) * upward).astype(BF)
        rests = jnp.zeros((64, COLS), F32)
        for c in range(GROUPS):
            down = w[c * 8:(c + 1) * 8, 2 * SHARD:, :].reshape(COLS, FF)
            res = lax.dot_general(hidden, down, (((1,), (1,)), ((), ())), preferred_element_type=F32).astype(BF)
            eout[pl.ds(base, 4), c * MAIN:(c + 1) * MAIN, :] = res[:4 * MAIN].reshape(4, MAIN, COLS)
            rests += jnp.dot(gather(c), res[4 * MAIN:], preferred_element_type=F32)
        eout[pl.ds(base, 4), GROUPS * MAIN:, :] = rests.astype(BF).reshape(4, 16, COLS)
        for dx in range(4):
            dy = hop_y((g + 1 + dx) % 4, dx)
            back_to = device((x + 4 - dx) % 4, (y + 8 - dy) % 8, z, core)
            if dx == 0:
                @pl.when(g < 3)
                def _():
                    message(base + dx, eout, back, ret_send, ret_recv, back_to).start()
            else:
                message(base + dx, eout, back, ret_send, ret_recv, back_to).start()
        return carry

    lax.fori_loop(0, 4, chunk, 0)
    back[12] = eout[12]
    pltpu.make_async_copy(back.at[0:15], back.at[0:15], ret_recv).wait()

    last = back[:, GROUPS * MAIN:, :].reshape(256, COLS)
    for c in range(GROUPS):
        main = back[:, c * MAIN:(c + 1) * MAIN, :].reshape(16 * MAIN, COLS)
        total = jnp.dot(whi[...], main, preferred_element_type=F32)
        total += jnp.dot(wlo[...], main, preferred_element_type=F32)
        total += jnp.dot(thi[c], last, preferred_element_type=F32)
        total += jnp.dot(tlo[c], last, preferred_element_type=F32)
        mixed_ref[:, c * COLS:(c + 1) * COLS] = tok[:, c * COLS:(c + 1) * COLS] + total

    @pl.when(home)
    def _():
        pltpu.make_async_copy(w.at[0], w.at[0], pre_send).wait()

    @pl.when(jnp.logical_not(home))
    def _():
        pltpu.make_async_copy(w.at[0:2], w.at[0:2], pre_send).wait()

    pltpu.make_async_copy(w.at[0:14], w.at[0:14], ring_send).wait()
    pltpu.make_async_copy(w.at[0:16], w.at[0:16], sib_send).wait()
    pltpu.make_async_copy(send.at[0:15], send.at[0:15], out_send).wait()
    pltpu.make_async_copy(eout.at[0:15], eout.at[0:15], ret_send).wait()


def on_device(tokens, expert_ids, combine_weights, gate_weight, up_weight, down_weight, norm_gain):
    anywhere = pl.BlockSpec(memory_space=pl.ANY)
    vmem = pl.BlockSpec(memory_space=pltpu.VMEM)
    dma = pltpu.SemaphoreType.DMA
    mixed = pl.pallas_call(
        kernel,
        out_shape=jax.ShapeDtypeStruct((TOK, WIDTH), F32),
        in_specs=[anywhere, vmem, vmem, vmem, anywhere, anywhere, anywhere],
        out_specs=vmem,
        scratch_shapes=[
            pltpu.VMEM((TOK, WIDTH), F32),
            pltpu.VMEM((32, PIECES * SHARD, FF), BF),
            pltpu.VMEM((16, ROWS, COLS), BF),
            pltpu.VMEM((16, ROWS, COLS), BF),
            pltpu.VMEM((16, ROWS, COLS), BF),
            pltpu.VMEM((16, ROWS, COLS), BF),
            pltpu.VMEM((TOK, 16 * MAIN), BF),
            pltpu.VMEM((TOK, 16 * MAIN), BF),
            pltpu.VMEM((GROUPS, TOK, 256), BF),
            pltpu.VMEM((GROUPS, TOK, 256), BF),
            dma, dma, dma((2, PIECES)), dma, dma((16 * PIECES,)), dma, dma((8,)),
            dma, dma, dma, dma,
        ],
        compiler_params=pltpu.CompilerParams(
            collective_id=0, has_side_effects=True, vmem_limit_bytes=48 << 20
        ),
        cost_estimate=pl.CostEstimate(flops=7_000_000_000, bytes_accessed=30_000_000, transcendentals=500_000),
    )(tokens, expert_ids, expert_ids.T, combine_weights, gate_weight, up_weight, down_weight)
    scale = lax.rsqrt(jnp.mean(mixed * mixed, axis=-1) + 1e-06)
    return mixed * scale[:, None] * norm_gain[None, :]


def solution(mesh):
    placed = (
        P(("replica", "expert"), None),
        P(("replica", "expert"), None),
        P(("replica", "expert"), None),
        P("expert", "replica", None),
        P("expert", "replica", None),
        P("expert", "replica", None),
        P(),
    )
    return jax.shard_map(
        on_device,
        mesh=mesh,
        in_specs=placed,
        out_specs=P(("replica", "expert"), None),
        check_vma=False,
    )
```

time: 248 us -> 120 us (0.48)
  the two profiles are of different devices: /device:TPU:1 before, /device:TPU:61 now
where the time goes in v1:
time: 120 us; the launch traced here: 119 us
  Pallas kernels  111 us (92%)
  local copies, waits for them, and re-layouts  6.85 us (6%)
  other arithmetic  1.53 us (1%)
    pallas_call x1, Pallas kernels, on_device(): pl.pallas_call(kernel, out_shape=jax.ShapeDtypeStruct((TOK, WIDTH), F32),...  111 us
    unnamed x14, local copies, waits for them, and re-layouts  6.85 us

profile of v1, /device:TPU:61, one launch (start us, length us, event | category | flops | bytes accessed | tf_op | source)
XLA Modules:
  0.0 119.3 jit_solution(16944989947408802942)
XLA Ops:
  0.0 0.8 copy.9.cw_ref
  0.8 0.8 copy.8.ids_ref
  1.6 0.0 copy-start
  1.6 0.7 copy-done
  2.3 0.0 copy-start.1
  2.3 1.4 %copy-done.1 = f32[192,2048]{1,0:T(8,128)S(1)} copy-done((f32[192,2048]{1,0:T(8,128)S(1)}, f32[192,2048]{1,0:T(8,128)}, u32[]{:S(2)}) %copy-start.1) | copy-done | bytes 1572888
  3.7 0.0 copy-start.2
  3.7 0.9 copy-done.2
  4.6 0.0 copy-start.3
  4.6 0.9 copy-done.3
  5.5 0.0 copy-start.4
  5.5 0.9 copy-done.4
  6.4 110.9 %shard_map.73 = f32[192,2048]{1,0:T(8,128)S(1)} custom-call(f32[192,2048]{1,0:T(8,128)S(1)} %copy-done.1, s32[192,2]{1,0:T(8,128)S(1)} %copy.8.ids_ref, s32[2,192]{1,0:T(2,128)S(1)} %bitcast.1, f32[192,2]{1,0:T(8,128)S(1)} %copy.9.cw_ref, bf16[1,64,768]{2,1,0:T(8,128)(2,1)S(1)} %copy-done.2, bf16[1,64,768]{2,1,0:T(8,128)(2,1)S(1)} %copy-done.3, ...), custom_call_target="tpu_custom_call" | custom-call | flops 7000000000 | bytes 30000000 | tf_op jit(solution)/shard_map/pallas_call | solution.py:289
  117.3 0.0 copy-start.5
  117.3 0.2 multiply_reduce_fusion
  117.5 0.5 copy-done.5
  118.0 1.3 %multiply_multiply_fusion = f32[192,2048]{1,0:T(8,128)} fusion(f32[192,2048]{1,0:T(8,128)S(1)} %shard_map.73, f32[2048]{0:T(1024)S(1)} %copy-done.5, f32[192]{0:T(256)S(1)} %add_rsqrt_fusion), kind=kLoop, calls=%fused_computation | loop fusion | flops 786432 | bytes 3154688 | tf_op jit(solution)/shard_map/mul | solution.py:314
  (1 shorter events, 0.0 us)
Async XLA Ops:
  1.6 0.7 copy-start
  2.3 1.4 %copy-start.1 = (f32[192,2048]{1,0:T(8,128)S(1)}, f32[192,2048]{1,0:T(8,128)}, u32[]{:S(2)}) copy-start(f32[192,2048]{1,0:T(8,128)} %tok_hbm.1) | copy-start | bytes 4718596
  3.7 0.9 copy-start.2
  4.6 0.9 copy-start.3
  5.5 0.9 copy-start.4
  117.3 0.7 copy-start.5

commit v2 on v1

v2 whole, which is shorter than its diff:
```python
import jax
import jax.numpy as jnp
from jax import lax
from jax.experimental import pallas as pl
from jax.experimental.pallas import tpu as pltpu
from jax.sharding import PartitionSpec as P

MESH = pl.DeviceIdType.MESH
BF = jnp.bfloat16
F32 = jnp.float32

TOK = 192
WIDTH = 2048
FF = 768
CAP = 36
MAIN = 32
TAIL = CAP - MAIN
GROUPS = 4
COLS = WIDTH // GROUPS
ROWS = GROUPS * CAP
SHARD = 64
PIECES = 3
SELF = 12


def hop_y(k, dx):
    far = 2 if dx < 2 else 6
    one = k * (2 - k) * (3 - k) // 2
    two = k * (k - 1) * (3 - k) // 2
    three = k * (k - 1) * (k - 2) // 6
    return one + 7 * two + far * three


def where_am_i():
    r = lax.axis_index("replica")
    e = lax.axis_index("expert")
    z = r // 4
    xh = (r // 2) % 2
    core = r % 2
    xl = e // 8
    y = e % 8
    return xh * 2 + xl, y, z, core


def device(x, y, z, core):
    return ((z * 2 + x // 2) * 2 + core, (x % 2) * 8 + y)


def partner_of(ids, x, y):
    host_x = (ids >> 3) + 2 * ((ids >> 2) & 1)
    dx = (host_x - x) & 3
    d4 = ((ids & 3) - y) & 3
    k = d4 ^ (d4 >> 1)
    return ((k - dx - 1) & 3) * 4 + dx


def iota(shape, dim):
    return lax.broadcasted_iota(jnp.int32, shape, dim)


def kernel(
    tok_hbm, ids_hbm, cw_hbm, gate_hbm, up_hbm, down_hbm,
    mixed_ref,
    tok, ids_ref, cw_ref, wgu, wd, send, recv, hid, eout, back, whi, wlo, thi, tlo,
    in_sem, pre_send, pre_recv, ring_send, ring_recv, down_recv, sib_send, sib_gu, sib_down,
    out_send, out_recv, ret_send, ret_recv,
):
    x, y, z, core = where_am_i()
    xh = x // 2
    mine = z * 4 + xh * 2 + core
    home = xh == y // 4
    shards = (gate_hbm, up_hbm, down_hbm)

    ids_copy = pltpu.make_async_copy(ids_hbm, ids_ref, in_sem.at[0])
    cw_copy = pltpu.make_async_copy(cw_hbm, cw_ref, in_sem.at[1])
    tok_copy = pltpu.make_async_copy(tok_hbm, tok, in_sem.at[2])
    ids_copy.start()
    cw_copy.start()
    tok_copy.start()

    offsets = [(dx, dy) for dx in range(4) for dy in (0, 1, 7)]
    offsets += [(0, 2), (0, 6), (1, 2), (2, 2), (2, 6), (3, 6)]
    offsets += [(0, 4), (2, 4)]
    greet = [device((x + dx) % 4, (y + dy) % 8, z, core) for dx, dy in offsets if (dx, dy) != (0, 0)]
    other = device(x, y, z, 1 - core)
    sides = (device(x, y, (z + 1) % 8, core), device(x, y, (z + 7) % 8, core))
    greet += [other, sides[0], sides[1]]
    barrier = pltpu.get_barrier_semaphore()
    for d in greet:
        pl.semaphore_signal(barrier, inc=1, device_id=d, device_id_type=MESH)
    pl.semaphore_wait(barrier, len(greet))

    def piece(slot, p):
        return wd.at[slot] if p == 2 else wgu.at[slot, pl.ds(p * SHARD, SHARD), :]

    def remote(src, dst, sem_from, sem_to, d):
        return pltpu.make_async_remote_copy(
            src_ref=src, dst_ref=dst, send_sem=sem_from, recv_sem=sem_to, device_id=d, device_id_type=MESH
        )

    def push_own(p, d):
        remote(shards[p].at[0], piece(mine, p), pre_send.at[p // 2], pre_recv.at[xh, p], d).start()

    @pl.when(home)
    def _():
        for p in range(PIECES):
            pltpu.make_async_copy(shards[p].at[0], piece(mine, p), pre_recv.at[xh, p]).start()
            push_own(p, device(x, (y + 4) % 8, z, core))

    @pl.when(jnp.logical_not(home))
    def _():
        for p in range(PIECES):
            push_own(p, device((x + 2) % 4, (y + 4) % 8, z, core))
            push_own(p, device((x + 2) % 4, y, z, core))

    ids_copy.wait()
    cw_copy.wait()
    tok_copy.wait()
    q0 = partner_of(ids_ref[0:1, :], x, y)
    q1 = partner_of(ids_ref[1:2, :], x, y)
    hot0 = (q0 == iota((16, TOK), 0)).astype(F32)
    hot1 = (q1 == iota((16, TOK), 0)).astype(F32)
    upper = (iota((TOK, TOK), 0) < iota((TOK, TOK), 1)).astype(BF)
    count = jnp.dot((hot0 + hot1).astype(BF), upper, preferred_element_type=F32)
    rank0 = jnp.sum(hot0 * count, axis=0, keepdims=True).astype(jnp.int32)
    rank1 = jnp.sum(hot1 * count, axis=0, keepdims=True).astype(jnp.int32)
    main0 = jnp.where(rank0 < MAIN, q0 * MAIN + rank0, -1)
    main1 = jnp.where(rank1 < MAIN, q1 * MAIN + rank1, -1)
    tail0 = jnp.where(rank0 < MAIN, -1000, q0 * 16 + rank0 - MAIN)
    tail1 = jnp.where(rank1 < MAIN, -1000, q1 * 16 + rank1 - MAIN)
    select = jnp.where((main0 == iota((16 * MAIN, TOK), 0)) | (main1 == iota((16 * MAIN, TOK), 0)), 1.0, 0.0).astype(BF)
    tails = jnp.zeros((256, COLS), F32)
    for c in range(GROUPS):
        tok_c = tok[:, c * COLS:(c + 1) * COLS].astype(BF)
        placed = jnp.dot(select, tok_c, preferred_element_type=F32).astype(BF)
        send[:, c * MAIN:(c + 1) * MAIN, :] = placed.reshape(16, MAIN, COLS)
        at = iota((256, TOK), 0) - 4 * c
        pick = jnp.where((tail0 == at) | (tail1 == at), 1.0, 0.0).astype(BF)
        tails += jnp.dot(pick, tok_c, preferred_element_type=F32)
    send[:, GROUPS * MAIN:, :] = tails.astype(BF).reshape(16, 16, COLS)

    partners = []
    for g in range(4):
        for dx in range(4):
            dy = hop_y((g + 1 + dx) % 4, dx)
            if (dx, dy) != (0, 0):
                partners.append((g * 4 + dx, dx, dy))
    for q, dx, dy in partners:
        remote(send.at[q], recv.at[q], out_send, out_recv, device((x + dx) % 4, (y + dy) % 8, z, core)).start()
    recv[SELF] = send[SELF]

    def arrival(step, way, hx, p):
        if p == 2:
            return down_recv.at[(step * 2 + way) * 2 + hx]
        return ring_recv.at[((step * 2 + way) * 2 + hx) * 2 + p]

    def onward(step, way, hx, p, slot):
        return remote(piece(slot, p), piece(slot, p), ring_send.at[p // 2], arrival(step, way, hx, p), sides[way])

    def sibling(p, slot, from_z):
        sem = sib_down.at[from_z] if p == 2 else sib_gu
        remote(piece(slot, p), piece(slot, p), sib_send.at[p // 2], sem, other).start()

    def own_turn(p):
        for turn in range(2):
            hx = xh if turn == 0 else 1 - xh
            slot = z * 4 + hx * 2 + core
            pltpu.make_async_copy(piece(slot, p), piece(slot, p), pre_recv.at[hx, p]).wait()
            for way in range(2):
                onward(0, way, hx, p, slot).start()
            sibling(p, slot, z)

    def ring_turn(step, pieces):
        for p in pieces:
            for hx in range(2):
                for way in range(2):
                    if step == 3 and way != hx:
                        continue
                    origin = (z + (7 - step if way == 0 else 1 + step)) % 8
                    slot = origin * 4 + hx * 2 + core
                    onward(step, way, hx, p, slot).wait_recv()
                    if step < 2 or (step == 2 and way == hx):
                        onward(step + 1, way, hx, p, slot).start()
                    sibling(p, slot, origin)

    own_turn(0)
    own_turn(1)
    ring_turn(0, (0, 1))

    diagonal = iota((TOK, TOK), 0) == iota((TOK, TOK), 1)

    def column(row):
        return jnp.sum(jnp.where(diagonal, row, 0.0), axis=1, keepdims=True)

    cw0 = column(cw_ref[0:1, :])
    cw1 = column(cw_ref[1:2, :])
    cmain0 = column(main0.astype(F32)).astype(jnp.int32)
    cmain1 = column(main1.astype(F32)).astype(jnp.int32)
    ctail0 = column(tail0.astype(F32)).astype(jnp.int32)
    ctail1 = column(tail1.astype(F32)).astype(jnp.int32)
    slots = iota((TOK, 16 * MAIN), 1)
    full = jnp.where(cmain0 == slots, cw0, 0.0) + jnp.where(cmain1 == slots, cw1, 0.0)
    high = full.astype(BF)
    whi[...] = high
    wlo[...] = (full - high.astype(F32)).astype(BF)
    for c in range(GROUPS):
        slots = iota((TOK, 256), 1) - 4 * c
        full = jnp.where(ctail0 == slots, cw0, 0.0) + jnp.where(ctail1 == slots, cw1, 0.0)
        high = full.astype(BF)
        thi[c] = high
        tlo[c] = (full - high.astype(F32)).astype(BF)

    ring_turn(1, (0, 1))
    ring_turn(2, (0, 1))
    own_turn(2)
    ring_turn(3, (0, 1))
    pltpu.make_async_copy(recv.at[0:15], recv.at[0:15], out_recv).wait()
    pltpu.make_async_copy(wgu.at[0:16], wgu.at[0:16], sib_gu).wait()

    def spread(c):
        a = iota((16, 64), 0)
        b = iota((16, 64), 1)
        return jnp.where((a // 4 == b // 16) & (a % 4 == b % 4) & ((b // 4) % 4 == c), 1.0, 0.0).astype(BF)

    def chunk(g, carry):
        base = pl.multiple_of(g * 4, 4)
        last = recv[pl.ds(base, 4), GROUPS * MAIN:, :].reshape(64, COLS)
        gate = jnp.zeros((4 * CAP, FF), F32)
        upward = jnp.zeros((4 * CAP, FF), F32)
        for c in range(GROUPS):
            main = recv[pl.ds(base, 4), c * MAIN:(c + 1) * MAIN, :].reshape(4 * MAIN, COLS)
            rest = jnp.dot(spread(c), last, preferred_element_type=F32).astype(BF)
            rows = jnp.concatenate([main, rest], axis=0)
            gate += jnp.dot(rows, wgu[c * 8:(c + 1) * 8, 0:SHARD, :].reshape(COLS, FF), preferred_element_type=F32)
            upward += jnp.dot(rows, wgu[c * 8:(c + 1) * 8, SHARD:, :].reshape(COLS, FF), preferred_element_type=F32)
        units = (gate / (1.0 + jnp.exp(-gate)) * upward).astype(BF)
        hid[pl.ds(pl.multiple_of(g * 128, 128), 128), :] = units[:128]
        hid[pl.ds(pl.multiple_of(512 + g * 16, 16), 16), :] = units[128:]
        return carry

    def pair(j):
        return ((z + (7 - j)) % 8, (z + 1 + j) % 8) if j < 3 else (z, (z + 4) % 8)

    def gather(s):
        a = iota((256, 64), 0)
        b = iota((256, 64), 1)
        return jnp.where((a // 16 == b // 4) & (a % 4 == b % 4) & ((a // 4) % 4 == s), 1.0, 0.0).astype(BF)

    def columns(j):
        rests = jnp.zeros((256, 128), F32)
        for half, origin in enumerate(pair(j)):
            pltpu.make_async_copy(wd.at[0:2], wd.at[0:2], sib_down.at[origin]).wait()
            down = wd[pl.ds(pl.multiple_of(origin * 4, 4), 4)].reshape(256, FF)
            res = lax.dot_general(hid[...], down, (((1,), (1,)), ((), ())), preferred_element_type=F32).astype(BF)
            for part in range(2):
                s = half * 2 + part
                lanes = res[:, part * 128:(part + 1) * 128]
                eout[j, :, s * MAIN:(s + 1) * MAIN, :] = lanes[:512].reshape(16, MAIN, 128)
                rests += jnp.dot(gather(s), lanes[512:], preferred_element_type=F32)
        eout[j, :, GROUPS * MAIN:, :] = rests.astype(BF).reshape(16, 16, 128)
        for q, dx, dy in partners:
            back_to = device((x + 4 - dx) % 4, (y + 8 - dy) % 8, z, core)
            remote(eout.at[j, q], back.at[j, q], ret_send.at[j], ret_recv.at[j], back_to).start()
        back[j, SELF] = eout[j, SELF]

    lax.fori_loop(0, 2, chunk, 0)
    ring_turn(0, (2,))
    lax.fori_loop(2, 4, chunk, 0)
    ring_turn(1, (2,))
    columns(0)
    ring_turn(2, (2,))
    columns(1)
    ring_turn(3, (2,))
    columns(2)
    columns(3)

    for j in range(4):
        pltpu.make_async_copy(back.at[j, 0:15], back.at[j, 0:15], ret_recv.at[j]).wait()
        last = back[j, :, GROUPS * MAIN:, :].reshape(256, 128)
        main = jnp.concatenate(
            [back[j, :, s * MAIN:(s + 1) * MAIN, :].reshape(16 * MAIN, 128) for s in range(4)], axis=1
        )
        total = jnp.dot(whi[...], main, preferred_element_type=F32)
        total += jnp.dot(wlo[...], main, preferred_element_type=F32)
        total += jnp.concatenate(
            [
                jnp.dot(thi[s], last, preferred_element_type=F32) + jnp.dot(tlo[s], last, preferred_element_type=F32)
                for s in range(4)
            ],
            axis=1,
        )
        for half, origin in enumerate(pair(j)):
            at = pl.ds(pl.multiple_of(origin * 256, 256), 256)
            mixed_ref[:, at] = tok[:, at] + total[:, half * 256:(half + 1) * 256]

    @pl.when(home)
    def _():
        pltpu.make_async_copy(wgu.at[0], wgu.at[0], pre_send.at[0]).wait()
        pltpu.make_async_copy(wd.at[0], wd.at[0], pre_send.at[1]).wait()

    @pl.when(jnp.logical_not(home))
    def _():
        pltpu.make_async_copy(wgu.at[0:2], wgu.at[0:2], pre_send.at[0]).wait()
        pltpu.make_async_copy(wd.at[0:2], wd.at[0:2], pre_send.at[1]).wait()

    pltpu.make_async_copy(wgu.at[0:14], wgu.at[0:14], ring_send.at[0]).wait()
    pltpu.make_async_copy(wd.at[0:14], wd.at[0:14], ring_send.at[1]).wait()
    pltpu.make_async_copy(wgu.at[0:16], wgu.at[0:16], sib_send.at[0]).wait()
    pltpu.make_async_copy(wd.at[0:16], wd.at[0:16], sib_send.at[1]).wait()
    pltpu.make_async_copy(send.at[0:15], send.at[0:15], out_send).wait()
    for j in range(4):
        pltpu.make_async_copy(eout.at[j, 0:15], eout.at[j, 0:15], ret_send.at[j]).wait()


def on_device(tokens, expert_ids, combine_weights, gate_weight, up_weight, down_weight, norm_gain):
    hbm = pl.BlockSpec(memory_space=pltpu.HBM)
    vmem = pl.BlockSpec(memory_space=pltpu.VMEM)
    dma = pltpu.SemaphoreType.DMA
    mixed = pl.pallas_call(
        kernel,
        out_shape=jax.ShapeDtypeStruct((TOK, WIDTH), F32),
        in_specs=[hbm] * 6,
        out_specs=vmem,
        scratch_shapes=[
            pltpu.VMEM((TOK, WIDTH), F32),
            pltpu.VMEM((2, TOK), jnp.int32),
            pltpu.VMEM((2, TOK), F32),
            pltpu.VMEM((32, 2 * SHARD, FF), BF),
            pltpu.VMEM((32, SHARD, FF), BF),
            pltpu.VMEM((16, ROWS, COLS), BF),
            pltpu.VMEM((16, ROWS, COLS), BF),
            pltpu.VMEM((16 * CAP, FF), BF),
            pltpu.VMEM((4, 16, ROWS, 128), BF),
            pltpu.VMEM((4, 16, ROWS, 128), BF),
            pltpu.VMEM((TOK, 16 * MAIN), BF),
            pltpu.VMEM((TOK, 16 * MAIN), BF),
            pltpu.VMEM((GROUPS, TOK, 256), BF),
            pltpu.VMEM((GROUPS, TOK, 256), BF),
            dma((3,)), dma((2,)), dma((2, PIECES)), dma((2,)), dma((32,)), dma((16,)), dma((2,)), dma, dma((8,)),
            dma, dma, dma((4,)), dma((4,)),
        ],
        compiler_params=pltpu.CompilerParams(
            collective_id=0, has_side_effects=True, vmem_limit_bytes=62500000
        ),
        cost_estimate=pl.CostEstimate(flops=7_000_000_000, bytes_accessed=30_000_000, transcendentals=500_000),
    )(tokens, expert_ids.T, combine_weights.T, gate_weight, up_weight, down_weight)
    scale = lax.rsqrt(jnp.mean(mixed * mixed, axis=-1) + 1e-06)
    return mixed * scale[:, None] * norm_gain[None, :]


def solution(mesh):
    placed = (
        P(("replica", "expert"), None),
        P(("replica", "expert"), None),
        P(("replica", "expert"), None),
        P("expert", "replica", None),
        P("expert", "replica", None),
        P("expert", "replica", None),
        P(),
    )
    return jax.shard_map(
        on_device,
        mesh=mesh,
        in_specs=placed,
        out_specs=P(("replica", "expert"), None),
        check_vma=False,
    )
```

time: 120 us -> 105 us (0.88)
  the two profiles are of different devices: /device:TPU:61 before, /device:TPU:1 now
where the time goes in v2:
time: 105 us; the launch traced here: 104 us
  Pallas kernels  101 us (96%)
  other arithmetic  3.06 us (3%)
    pallas_call x1, Pallas kernels, on_device(): pl.pallas_call(kernel, out_shape=jax.ShapeDtypeStruct((TOK, WIDTH), F32),...  101 us

profile of v2, /device:TPU:1, one launch (start us, length us, event | category | flops | bytes accessed | tf_op | source)
XLA Modules:
  0.0 104.2 jit_solution(7594823709567983903)
XLA Ops:
  0.0 0.0 copy-start.1
  0.0 101.0 %shard_map.73 = f32[192,2048]{1,0:T(8,128)} custom-call(f32[192,2048]{1,0:T(8,128)} %tok_hbm.1, s32[2,192]{1,0:T(2,128)} %bitcast.2, f32[2,192]{1,0:T(2,128)} %bitcast.3, bf16[1,64,768]{2,1,0:T(8,128)(2,1)} %gate_hbm.1, bf16[1,64,768]{2,1,0:T(8,128)(2,1)} %up_hbm.1, bf16[1,64,768]{2,1,0:T(8,128)(2,1)} %down_hbm.1), custom_call_target="tpu_custom_call" | custom-call | flops 7000000000 | bytes 30000000 | tf_op jit(solution)/shard_map/pallas_call | solution.py:319
  101.0 0.0 copy-start
  101.0 1.7 %multiply_reduce_fusion = f32[192]{0:T(256)S(1)} fusion(f32[192,2048]{1,0:T(8,128)} %shard_map.73), kind=kLoop, calls=%fused_computation.1 | loop fusion | flops 786240 | bytes 1573632 | tf_op jit(solution)/shard_map/reduce_sum | solution.py:347
  102.7 0.0 copy-done.1
  102.7 0.1 copy-done
  102.9 1.3 %multiply_multiply_fusion = f32[192,2048]{1,0:T(8,128)} fusion(f32[192,2048]{1,0:T(8,128)S(1)} %copy-done, f32[2048]{0:T(1024)S(1)} %copy-done.1, f32[192]{0:T(256)S(1)} %add_rsqrt_fusion), kind=kLoop, calls=%fused_computation | loop fusion | flops 786432 | bytes 3154688 | tf_op jit(solution)/shard_map/mul | solution.py:348
  (1 shorter events, 0.0 us)
Async XLA Ops:
  0.0 102.7 %copy-start.1 = (f32[2048]{0:T(1024)S(1)}, f32[2048]{0:T(1024)}, u32[]{:S(2)}) copy-start(f32[2048]{0:T(1024)} %param.13) | copy-start | bytes 24580
  101.0 1.9 %copy-start = (f32[192,2048]{1,0:T(8,128)S(1)}, f32[192,2048]{1,0:T(8,128)}, u32[]{:S(2)}) copy-start(f32[192,2048]{1,0:T(8,128)} %shard_map.73) | copy-start | bytes 4718596

commit v3 on v2

--- a/solution.py
+++ b/solution.py
@@ -21,6 +21,9 @@
 SHARD = 64
 PIECES = 3
 SELF = 12
+HALF = 8 * CAP
+HALF_MAIN = 8 * MAIN
+HALF_TAIL = 8 * TAIL
 
 
 def hop_y(k, dx):
@@ -60,9 +63,9 @@
 
 def kernel(
     tok_hbm, ids_hbm, cw_hbm, gate_hbm, up_hbm, down_hbm,
-    mixed_ref,
-    tok, ids_ref, cw_ref, wgu, wd, send, recv, hid, eout, back, whi, wlo, thi, tlo,
-    in_sem, pre_send, pre_recv, ring_send, ring_recv, down_recv, sib_send, sib_gu, sib_down,
+    mixed_hbm, scale_ref,
+    tok, ids_ref, cw_ref, wgu, wd, send, recv, lhs, gacc, uacc, hid, eout, back, whi, wlo, thi, tlo,
+    in_sem, res_sem, pre_send, pre_recv, ring_send, ring_recv, down_recv, sib_send, sib_gu, sib_down,
     out_send, out_recv, ret_send, ret_recv,
 ):
     x, y, z, core = where_am_i()
@@ -146,7 +149,7 @@
             if (dx, dy) != (0, 0):
                 partners.append((g * 4 + dx, dx, dy))
     for q, dx, dy in partners:
-        remote(send.at[q], recv.at[q], out_send, out_recv, device((x + dx) % 4, (y + dy) % 8, z, core)).start()
+        remote(send.at[q], recv.at[q], out_send, out_recv.at[q // 8], device((x + dx) % 4, (y + dy) % 8, z, core)).start()
     recv[SELF] = send[SELF]
 
     def arrival(step, way, hx, p):
@@ -158,7 +161,7 @@
         return remote(piece(slot, p), piece(slot, p), ring_send.at[p // 2], arrival(step, way, hx, p), sides[way])
 
     def sibling(p, slot, from_z):
-        sem = sib_down.at[from_z] if p == 2 else sib_gu
+        sem = sib_down.at[from_z] if p == 2 else sib_gu.at[from_z]
         remote(piece(slot, p), piece(slot, p), sib_send.at[p // 2], sem, other).start()
 
     def own_turn(p):
@@ -210,70 +213,97 @@
         thi[c] = high
         tlo[c] = (full - high.astype(F32)).astype(BF)
 
+    def spread(c):
+        a = iota((HALF_TAIL, 128), 0)
+        b = iota((HALF_TAIL, 128), 1)
+        return jnp.where((a // 4 == b // 16) & (a % 4 == b % 4) & ((b // 4) % 4 == c), 1.0, 0.0).astype(BF)
+
+    def unpack(h):
+        got = recv.at[0:8 - h]
+        pltpu.make_async_copy(got, got, out_recv.at[h]).wait()
+        last = recv[h * 8:h * 8 + 8, GROUPS * MAIN:, :].reshape(128, COLS)
+        for c in range(GROUPS):
+            main = recv[h * 8:h * 8 + 8, c * MAIN:(c + 1) * MAIN, :].reshape(HALF_MAIN, COLS)
+            rest = jnp.dot(spread(c), last, preferred_element_type=F32).astype(BF)
+            for part in range(2):
+                lanes = slice(part * 256, (part + 1) * 256)
+                lhs[c * 2 + part, h * HALF:h * HALF + HALF_MAIN, :] = main[:, lanes]
+                lhs[c * 2 + part, h * HALF + HALF_MAIN:(h + 1) * HALF, :] = rest[:, lanes]
+
+    def weights_of(origin, p):
+        at = pl.ds(pl.multiple_of(origin * 4, 4), 4)
+        return wgu[at, p * SHARD:(p + 1) * SHARD, :].reshape(256, FF)
+
+    def product(h, p, origins):
+        rows = jnp.concatenate([lhs[o, h * HALF:(h + 1) * HALF, :] for o in origins], axis=1)
+        return jnp.dot(rows, jnp.concatenate([weights_of(o, p) for o in origins], axis=0), preferred_element_type=F32)
+
+    def activate(h, gate, upward):
+        hid[h * HALF:(h + 1) * HALF, :] = (gate / (1.0 + jnp.exp(-gate)) * upward).astype(BF)
+
+    def crossed(origin):
+        pltpu.make_async_copy(wgu.at[0:2], wgu.at[0:2], sib_gu.at[origin]).wait()
+
+    def pair(j):
+        return ((z + (7 - j)) % 8, (z + 1 + j) % 8) if j < 3 else (z, (z + 4) % 8)
+
+    def gather(s):
+        a = iota((128, HALF_TAIL), 0)
+        b = iota((128, HALF_TAIL), 1)
+        return jnp.where((a // 16 == b // 4) & (a % 4 == b % 4) & ((a // 4) % 4 == s), 1.0, 0.0).astype(BF)
+
+    def columns(j, h):
+        rests = jnp.zeros((128, 128), F32)
+        for half, origin in enumerate(pair(j)):
+            if h == 0:
+                pltpu.make_async_copy(wd.at[0:2], wd.at[0:2], sib_down.at[origin]).wait()
+            down = wd[pl.ds(pl.multiple_of(origin * 4, 4), 4)].reshape(256, FF)
+            res = lax.dot_general(
+                hid[h * HALF:(h + 1) * HALF, :], down, (((1,), (1,)), ((), ())), preferred_element_type=F32
+            ).astype(BF)
+            for part in range(2):
+                s = half * 2 + part
+                lanes = res[:, part * 128:(part + 1) * 128]
+                eout[j, h * 8:h * 8 + 8, s * MAIN:(s + 1) * MAIN, :] = lanes[:HALF_MAIN].reshape(8, MAIN, 128)
+                rests += jnp.dot(gather(s), lanes[HALF_MAIN:], preferred_element_type=F32)
+        eout[j, h * 8:h * 8 + 8, GROUPS * MAIN:, :] = rests.astype(BF).reshape(8, 16, 128)
+        for q, dx, dy in partners:
+            if q // 8 == h:
+                back_to = device((x + 4 - dx) % 4, (y + 8 - dy) % 8, z, core)
+                remote(eout.at[j, q], back.at[j, q], ret_send.at[j], ret_recv.at[j], back_to).start()
+        if h == SELF // 8:
+            back[j, SELF] = eout[j, SELF]
+
     ring_turn(1, (0, 1))
     ring_turn(2, (0, 1))
     own_turn(2)
+    near = [z, (z + 7) % 8, (z + 1) % 8, (z + 6) % 8, (z + 2) % 8, (z + 5) % 8, (z + 3) % 8]
+    opposite = (z + 4) % 8
+    for origin in near:
+        crossed(origin)
+    unpack(0)
+    gacc[...] = product(0, 0, near)
+    uacc[...] = product(0, 1, near)
     ring_turn(3, (0, 1))
-    pltpu.make_async_copy(recv.at[0:15], recv.at[0:15], out_recv).wait()
-    pltpu.make_async_copy(wgu.at[0:16], wgu.at[0:16], sib_gu).wait()
-
-    def spread(c):
-        a = iota((16, 64), 0)
-        b = iota((16, 64), 1)
-        return jnp.where((a // 4 == b // 16) & (a % 4 == b % 4) & ((b // 4) % 4 == c), 1.0, 0.0).astype(BF)
-
-    def chunk(g, carry):
-        base = pl.multiple_of(g * 4, 4)
-        last = recv[pl.ds(base, 4), GROUPS * MAIN:, :].reshape(64, COLS)
-        gate = jnp.zeros((4 * CAP, FF), F32)
-        upward = jnp.zeros((4 * CAP, FF), F32)
-        for c in range(GROUPS):
-            main = recv[pl.ds(base, 4), c * MAIN:(c + 1) * MAIN, :].reshape(4 * MAIN, COLS)
-            rest = jnp.dot(spread(c), last, preferred_element_type=F32).astype(BF)
-            rows = jnp.concatenate([main, rest], axis=0)
-            gate += jnp.dot(rows, wgu[c * 8:(c + 1) * 8, 0:SHARD, :].reshape(COLS, FF), preferred_element_type=F32)
-            upward += jnp.dot(rows, wgu[c * 8:(c + 1) * 8, SHARD:, :].reshape(COLS, FF), preferred_element_type=F32)
-        units = (gate / (1.0 + jnp.exp(-gate)) * upward).astype(BF)
-        hid[pl.ds(pl.multiple_of(g * 128, 128), 128), :] = units[:128]
-        hid[pl.ds(pl.multiple_of(512 + g * 16, 16), 16), :] = units[128:]
-        return carry
-
-    def pair(j):
-        return ((z + (7 - j)) % 8, (z + 1 + j) % 8) if j < 3 else (z, (z + 4) % 8)
-
-    def gather(s):
-        a = iota((256, 64), 0)
-        b = iota((256, 64), 1)
-        return jnp.where((a // 16 == b // 4) & (a % 4 == b % 4) & ((a // 4) % 4 == s), 1.0, 0.0).astype(BF)
-
-    def columns(j):
-        rests = jnp.zeros((256, 128), F32)
-        for half, origin in enumerate(pair(j)):
-            pltpu.make_async_copy(wd.at[0:2], wd.at[0:2], sib_down.at[origin]).wait()
-            down = wd[pl.ds(pl.multiple_of(origin * 4, 4), 4)].reshape(256, FF)
-            res = lax.dot_general(hid[...], down, (((1,), (1,)), ((), ())), preferred_element_type=F32).astype(BF)
-            for part in range(2):
-                s = half * 2 + part
-                lanes = res[:, part * 128:(part + 1) * 128]
-                eout[j, :, s * MAIN:(s + 1) * MAIN, :] = lanes[:512].reshape(16, MAIN, 128)
-                rests += jnp.dot(gather(s), lanes[512:], preferred_element_type=F32)
-        eout[j, :, GROUPS * MAIN:, :] = rests.astype(BF).reshape(16, 16, 128)
-        for q, dx, dy in partners:
-            back_to = device((x + 4 - dx) % 4, (y + 8 - dy) % 8, z, core)
-            remote(eout.at[j, q], back.at[j, q], ret_send.at[j], ret_recv.at[j], back_to).start()
-        back[j, SELF] = eout[j, SELF]
-
-    lax.fori_loop(0, 2, chunk, 0)
+    crossed(opposite)
+    activate(0, gacc[...] + product(0, 0, [opposite]), uacc[...] + product(0, 1, [opposite]))
     ring_turn(0, (2,))
-    lax.fori_loop(2, 4, chunk, 0)
+    columns(0, 0)
+    unpack(1)
+    gacc[...] = product(1, 0, near + [opposite])
+    activate(1, gacc[...], product(1, 1, near + [opposite]))
+    columns(0, 1)
     ring_turn(1, (2,))
-    columns(0)
+    columns(1, 0)
+    columns(1, 1)
     ring_turn(2, (2,))
-    columns(1)
+    columns(2, 0)
+    columns(2, 1)
     ring_turn(3, (2,))
-    columns(2)
-    columns(3)
-
+    columns(3, 0)
+    columns(3, 1)
+
+    squares = jnp.zeros((TOK, 1), F32)
     for j in range(4):
         pltpu.make_async_copy(back.at[j, 0:15], back.at[j, 0:15], ret_recv.at[j]).wait()
         last = back[j, :, GROUPS * MAIN:, :].reshape(256, 128)
@@ -291,7 +321,12 @@
         )
         for half, origin in enumerate(pair(j)):
             at = pl.ds(pl.multiple_of(origin * 256, 256), 256)
-            mixed_ref[:, at] = tok[:, at] + total[:, half * 256:(half + 1) * 256]
+            mixed = tok[:, at] + total[:, half * 256:(half + 1) * 256]
+            squares += jnp.sum(mixed * mixed, axis=1, keepdims=True)
+            tok[:, at] = mixed
+            pltpu.make_async_copy(tok.at[:, at], mixed_hbm.at[:, at], res_sem).start()
+    scale_ref[...] = lax.rsqrt(squares * (1.0 / WIDTH) + 1e-06)
+    pltpu.make_async_copy(tok, mixed_hbm, res_sem).wait()
 
     @pl.when(home)
     def _():
@@ -316,11 +351,11 @@
     hbm = pl.BlockSpec(memory_space=pltpu.HBM)
     vmem = pl.BlockSpec(memory_space=pltpu.VMEM)
     dma = pltpu.SemaphoreType.DMA
-    mixed = pl.pallas_call(
+    mixed, scale = pl.pallas_call(
         kernel,
-        out_shape=jax.ShapeDtypeStruct((TOK, WIDTH), F32),
+        out_shape=(jax.ShapeDtypeStruct((TOK, WIDTH), F32), jax.ShapeDtypeStruct((TOK, 1), F32)),
         in_specs=[hbm] * 6,
-        out_specs=vmem,
+        out_specs=(hbm, vmem),
         scratch_shapes=[
             pltpu.VMEM((TOK, WIDTH), F32),
             pltpu.VMEM((2, TOK), jnp.int32),
@@ -329,6 +364,9 @@
             pltpu.VMEM((32, SHARD, FF), BF),
             pltpu.VMEM((16, ROWS, COLS), BF),
             pltpu.VMEM((16, ROWS, COLS), BF),
+            pltpu.VMEM((8, 16 * CAP, 256), BF),
+            pltpu.VMEM((HALF, FF), F32),
+            pltpu.VMEM((HALF, FF), F32),
             pltpu.VMEM((16 * CAP, FF), BF),
             pltpu.VMEM((4, 16, ROWS, 128), BF),
             pltpu.VMEM((4, 16, ROWS, 128), BF),
@@ -336,16 +374,15 @@
             pltpu.VMEM((TOK, 16 * MAIN), BF),
             pltpu.VMEM((GROUPS, TOK, 256), BF),
             pltpu.VMEM((GROUPS, TOK, 256), BF),
-            dma((3,)), dma((2,)), dma((2, PIECES)), dma((2,)), dma((32,)), dma((16,)), dma((2,)), dma, dma((8,)),
-            dma, dma, dma((4,)), dma((4,)),
+            dma((3,)), dma, dma((2,)), dma((2, PIECES)), dma((2,)), dma((32,)), dma((16,)), dma((2,)), dma((8,)), dma((8,)),
+            dma, dma((2,)), dma((4,)), dma((4,)),
         ],
         compiler_params=pltpu.CompilerParams(
             collective_id=0, has_side_effects=True, vmem_limit_bytes=62500000
         ),
         cost_estimate=pl.CostEstimate(flops=7_000_000_000, bytes_accessed=30_000_000, transcendentals=500_000),
     )(tokens, expert_ids.T, combine_weights.T, gate_weight, up_weight, down_weight)
-    scale = lax.rsqrt(jnp.mean(mixed * mixed, axis=-1) + 1e-06)
-    return mixed * scale[:, None] * norm_gain[None, :]
+    return mixed * scale * norm_gain[None, :]
 
 
 def solution(mesh):

time: 105 us -> 97.5 us (0.929); the launches traced: 104 us -> 95.5 us
  Pallas kernels: 101 us -> 91.8 us
    pallas_call x1, Pallas kernels: 101 us -> 91.8 us  [on_device(): pl.pallas_call(kernel, out_shape=(jax.ShapeDtypeStruct((TOK, WIDTH), F32)...]
    reduce_sum x1 -> x0, other arithmetic: 1.71 us -> none  [on_device(): scale = lax.rsqrt(jnp.mean(mixed * mixed, axis=-1) + 1e-06)]
    mul x1, other arithmetic: 1.34 us -> 2.75 us  [on_device(): return mixed * scale * norm_gain[None, :]]
where the time goes in v3:
time: 97.5 us; the launch traced here: 95.5 us
  Pallas kernels  91.8 us (94%)
  other arithmetic  3.74 us (4%)
    pallas_call x1, Pallas kernels, on_device(): pl.pallas_call(kernel, out_shape=(jax.ShapeDtypeStruct((TOK, WIDTH), F32)...  91.8 us
    mul x1, other arithmetic, on_device(): return mixed * scale * norm_gain[None, :]  2.75 us

profile of v3, /device:TPU:1, one launch (start us, length us, event | category | flops | bytes accessed | tf_op | source)
XLA Modules:
  0.0 95.5 jit_solution(7549679800905948423)
XLA Ops:
  0.0 0.0 copy-start
  0.0 91.8 %shard_map.73 = (f32[192,2048]{1,0:T(8,128)}, f32[192,1]{1,0:T(8,128)}) custom-call(f32[192,2048]{1,0:T(8,128)} %tok_hbm.1, s32[2,192]{1,0:T(2,128)} %bitcast.2, f32[2,192]{1,0:T(2,128)} %bitcast.3, bf16[1,64,768]{2,1,0:T(8,128)(2,1)} %gate_hbm.1, bf16[1,64,768]{2,1,0:T(8,128)(2,1)} %up_hbm.1, bf16[1,64,768]{2,1,0:T(8,128)(2,1)} %down_hbm.1), custom_call_target="tpu_custom_call" | custom-call | flops 7000000000 | bytes 30000000 | tf_op jit(solution)/shard_map/pallas_call | solution.py:354
  91.8 1.0 %reduce = f32[192]{0:T(256)S(1)} reduce(f32[192,1]{1,0:T(8,128)} %get-tuple-element.8, f32[]{:T(128)} %constant.6), dimensions={1}, to_apply=%get-tuple-element.8.reduce_sub_computation | reduce | bytes 1540 | tf_op jit(solution)/shard_map/pallas_call | solution.py:354
  92.8 0.0 copy-done
  92.8 2.7 %multiply_multiply_fusion = f32[192,2048]{1,0:T(8,128)} fusion(f32[192,2048]{1,0:T(8,128)} %get-tuple-element.7, f32[2048]{0:T(1024)S(1)} %copy-done, f32[192]{0:T(256)S(1)} %reduce), kind=kLoop, calls=%fused_computation | loop fusion | flops 786432 | bytes 3154688 | tf_op jit(solution)/shard_map/mul | solution.py:385
Async XLA Ops:
  0.0 92.8 %copy-start = (f32[2048]{0:T(1024)S(1)}, f32[2048]{0:T(1024)}, u32[]{:S(2)}) copy-start(f32[2048]{0:T(1024)} %param.13) | copy-start | bytes 24580

commit v4 on v3

--- a/solution.py
+++ b/solution.py
@@ -62,10 +62,10 @@
 
 
 def kernel(
-    tok_hbm, ids_hbm, cw_hbm, gate_hbm, up_hbm, down_hbm,
-    mixed_hbm, scale_ref,
-    tok, ids_ref, cw_ref, wgu, wd, send, recv, lhs, gacc, uacc, hid, eout, back, whi, wlo, thi, tlo,
-    in_sem, res_sem, pre_send, pre_recv, ring_send, ring_recv, down_recv, sib_send, sib_gu, sib_down,
+    tok_hbm, ids_hbm, cw_hbm, gate_hbm, up_hbm, down_hbm, gain_hbm,
+    out_ref,
+    tok, ids_ref, cw_ref, gain_ref, wgu, wd, send, recv, lhs, gacc, uacc, hid, eout, back, whi, wlo, thi, tlo,
+    in_sem, pre_send, pre_recv, ring_send, ring_recv, down_recv, sib_send, sib_gu, sib_down,
     out_send, out_recv, ret_send, ret_recv,
 ):
     x, y, z, core = where_am_i()
@@ -80,6 +80,8 @@
     ids_copy.start()
     cw_copy.start()
     tok_copy.start()
+    gain_copy = pltpu.make_async_copy(gain_hbm, gain_ref, in_sem.at[3])
+    gain_copy.start()
 
     offsets = [(dx, dy) for dx in range(4) for dy in (0, 1, 7)]
     offsets += [(0, 2), (0, 6), (1, 2), (2, 2), (2, 6), (3, 6)]
@@ -119,6 +121,7 @@
     ids_copy.wait()
     cw_copy.wait()
     tok_copy.wait()
+    gain_copy.wait()
     q0 = partner_of(ids_ref[0:1, :], x, y)
     q1 = partner_of(ids_ref[1:2, :], x, y)
     hot0 = (q0 == iota((16, TOK), 0)).astype(F32)
@@ -323,10 +326,11 @@
             at = pl.ds(pl.multiple_of(origin * 256, 256), 256)
             mixed = tok[:, at] + total[:, half * 256:(half + 1) * 256]
             squares += jnp.sum(mixed * mixed, axis=1, keepdims=True)
-            tok[:, at] = mixed
-            pltpu.make_async_copy(tok.at[:, at], mixed_hbm.at[:, at], res_sem).start()
-    scale_ref[...] = lax.rsqrt(squares * (1.0 / WIDTH) + 1e-06)
-    pltpu.make_async_copy(tok, mixed_hbm, res_sem).wait()
+            out_ref[:, at] = mixed
+    scale = lax.rsqrt(squares * (1.0 / WIDTH) + 1e-06)
+    for c in range(GROUPS):
+        lanes = slice(c * COLS, (c + 1) * COLS)
+        out_ref[:, lanes] = out_ref[:, lanes] * scale * gain_ref[:, lanes]
 
     @pl.when(home)
     def _():
@@ -351,15 +355,16 @@
     hbm = pl.BlockSpec(memory_space=pltpu.HBM)
     vmem = pl.BlockSpec(memory_space=pltpu.VMEM)
     dma = pltpu.SemaphoreType.DMA
-    mixed, scale = pl.pallas_call(
+    return pl.pallas_call(
         kernel,
-        out_shape=(jax.ShapeDtypeStruct((TOK, WIDTH), F32), jax.ShapeDtypeStruct((TOK, 1), F32)),
-        in_specs=[hbm] * 6,
-        out_specs=(hbm, vmem),
+        out_shape=jax.ShapeDtypeStruct((TOK, WIDTH), F32),
+        in_specs=[hbm] * 7,
+        out_specs=vmem,
         scratch_shapes=[
             pltpu.VMEM((TOK, WIDTH), F32),
             pltpu.VMEM((2, TOK), jnp.int32),
             pltpu.VMEM((2, TOK), F32),
+            pltpu.VMEM((1, WIDTH), F32),
             pltpu.VMEM((32, 2 * SHARD, FF), BF),
             pltpu.VMEM((32, SHARD, FF), BF),
             pltpu.VMEM((16, ROWS, COLS), BF),
@@ -374,15 +379,14 @@
             pltpu.VMEM((TOK, 16 * MAIN), BF),
             pltpu.VMEM((GROUPS, TOK, 256), BF),
             pltpu.VMEM((GROUPS, TOK, 256), BF),
-            dma((3,)), dma, dma((2,)), dma((2, PIECES)), dma((2,)), dma((32,)), dma((16,)), dma((2,)), dma((8,)), dma((8,)),
+            dma((4,)), dma((2,)), dma((2, PIECES)), dma((2,)), dma((32,)), dma((16,)), dma((2,)), dma((8,)), dma((8,)),
             dma, dma((2,)), dma((4,)), dma((4,)),
         ],
         compiler_params=pltpu.CompilerParams(
-            collective_id=0, has_side_effects=True, vmem_limit_bytes=62500000
+            collective_id=0, has_side_effects=True, vmem_limit_bytes=48000000
         ),
         cost_estimate=pl.CostEstimate(flops=7_000_000_000, bytes_accessed=30_000_000, transcendentals=500_000),
-    )(tokens, expert_ids.T, combine_weights.T, gate_weight, up_weight, down_weight)
-    return mixed * scale * norm_gain[None, :]
+    )(*[pltpu.with_memory_space_constraint(v, pltpu.HBM) for v in (tokens, expert_ids.T, combine_weights.T, gate_weight, up_weight, down_weight, norm_gain[None, :])])
 
 
 def solution(mesh):

time: 97.5 us -> 93.5 us (0.959)
  the two profiles are of different devices: /device:TPU:1 before, /device:TPU:3 now
where the time goes in v4:
time: 93.5 us; the launch traced here: 93.3 us
  Pallas kernels  92.2 us (99%)
  local copies, waits for them, and re-layouts  1.15 us (1%)
    pallas_call x1, Pallas kernels, on_device(): pl.pallas_call(kernel, out_shape=jax.ShapeDtypeStruct((TOK, WIDTH), F32),...  92.2 us

profile of v4, /device:TPU:3, one launch (start us, length us, event | category | flops | bytes accessed | tf_op | source)
XLA Modules:
  0.0 93.3 jit_solution(13756704959365680227)
XLA Ops:
  0.0 92.2 %shard_map.73 = f32[192,2048]{1,0:T(8,128)S(1)} custom-call(f32[192,2048]{1,0:T(8,128)} %tok_hbm.1, s32[2,192]{1,0:T(2,128)} %bitcast.4, f32[2,192]{1,0:T(2,128)} %bitcast.5, bf16[1,64,768]{2,1,0:T(8,128)(2,1)} %gate_hbm.1, bf16[1,64,768]{2,1,0:T(8,128)(2,1)} %up_hbm.1, bf16[1,64,768]{2,1,0:T(8,128)(2,1)} %down_hbm.1, f32[1,2048]{1,0:T(1,128)} %bitcast.3), custom_call_target="tpu_custom_call" | custom-call | flops 7000000000 | bytes 30000000 | tf_op jit(solution)/shard_map/pallas_call | solution.py:358
  92.2 1.1 %copy.9 = f32[192,2048]{1,0:T(8,128)} copy(f32[192,2048]{1,0:T(8,128)S(1)} %shard_map.73) | data formatting | bytes 3145728

commit v5 on v4

--- a/solution.py
+++ b/solution.py
@@ -151,6 +151,8 @@
             dy = hop_y((g + 1 + dx) % 4, dx)
             if (dx, dy) != (0, 0):
                 partners.append((g * 4 + dx, dx, dy))
+    partners.sort(key=lambda m: (min(m[1], 4 - m[1]), -min(m[2], 8 - m[2])))
+    partners = [partners[i // 2] if i % 2 == 0 else partners[-1 - i // 2] for i in range(len(partners))]
     for q, dx, dy in partners:
         remote(send.at[q], recv.at[q], out_send, out_recv.at[q // 8], device((x + dx) % 4, (y + dy) % 8, z, core)).start()
     recv[SELF] = send[SELF]

time: 93.5 us -> 95.3 us (1.019)
  the two profiles are of different devices: /device:TPU:3 before, /device:TPU:1 now
where the time goes in v5:
time: 95.3 us; the launch traced here: 95.2 us
  Pallas kernels  94 us (99%)
  local copies, waits for them, and re-layouts  1.15 us (1%)
    pallas_call x1, Pallas kernels, on_device(): pl.pallas_call(kernel, out_shape=jax.ShapeDtypeStruct((TOK, WIDTH), F32),...  94 us

profile of v5, /device:TPU:1, one launch (start us, length us, event | category | flops | bytes accessed | tf_op | source)
XLA Modules:
  0.0 95.2 jit_solution(4387069792394500077)
XLA Ops:
  0.0 94.0 %shard_map.73 = f32[192,2048]{1,0:T(8,128)S(1)} custom-call(f32[192,2048]{1,0:T(8,128)} %tok_hbm.1, s32[2,192]{1,0:T(2,128)} %bitcast.4, f32[2,192]{1,0:T(2,128)} %bitcast.5, bf16[1,64,768]{2,1,0:T(8,128)(2,1)} %gate_hbm.1, bf16[1,64,768]{2,1,0:T(8,128)(2,1)} %up_hbm.1, bf16[1,64,768]{2,1,0:T(8,128)(2,1)} %down_hbm.1, f32[1,2048]{1,0:T(1,128)} %bitcast.3), custom_call_target="tpu_custom_call" | custom-call | flops 7000000000 | bytes 30000000 | tf_op jit(solution)/shard_map/pallas_call | solution.py:360
  94.0 1.1 %copy.9 = f32[192,2048]{1,0:T(8,128)} copy(f32[192,2048]{1,0:T(8,128)S(1)} %shard_map.73) | data formatting | bytes 3145728
